TPU v7x, 32 devices: a whole 2x2x4 slice. The times are simulated.
32 devices in a mesh: parts: 2 (over y), row: 4 (over z), col: 4 (over x, core).
Axes of the slice: x: 2, y: 2, z: 4, core: 2. Of those that a mesh axis runs over, the one named last changes fastest.
Arguments:
- state: float32 [10, 128, 512], P(None, ('parts', 'row'), 'col'), parts along dimension 1, may hold values from -5 to 5
- history: float32 [10, 128, 512], P(None, ('parts', 'row'), 'col'), parts along dimension 1, may hold values from -5 to 5
- rates: float32 [10, 10, 128, 512], P(None, None, ('parts', 'row'), 'col'), parts along dimension 2, may hold values from -2 to 2
- quadratic: float32 [10, 128, 512], P(None, ('parts', 'row'), 'col'), parts along dimension 1, may hold values from 0.1 to 1
- velocity: float32 [10, 2], replicated, may hold values from -1.5 to 1.5
- precond: float32 [10, 10, 128, 512], P(None, None, ('parts', 'row'), 'col'), parts along dimension 2, may hold values from -1 to 2, as said below
Outputs:
- updated: float32 [10, 128, 512], P(None, ('parts', 'row'), 'col'), parts along dimension 1
- lin_residual: float32 [2], P('parts'), parts along dimension 0
There are 2 independent parts, one for each index of `parts`. A program takes and returns all parts, laid end to end along the dimension named above; an argument that names none is the same for every part. Nothing has to cross between parts.
Inputs may be any that keep to these rules, and one draw needn't show every extreme that they name: `precond`: each cell's block has diagonal entries 1 plus a spread term and independent off-diagonal entries.
All inputs are finite; a program needn't handle non-finite values.
Results may differ from a plain program's by a relative error of at most 0.00011.
Values sent between devices are 32-bit elements; how exact they have to be, the bound alone decides.
No kernel may reach another device: no remote copies, remote signals or barrier semaphores. Data moves between devices by JAX's collectives and lax.ppermute only.
A program may use at most 64 MiB of HBM per device.

v0:
```python
import jax
import jax.numpy as jnp
from jax import lax
from jax.sharding import PartitionSpec as P

KRYLOV = 4
step_gamma = 0.4
tiny_eps = 1e-12


def extended(block, sides, width):
    for axis, dim in sides:
        count = lax.axis_size(axis)
        forward = [(i, i + 1) for i in range(count - 1)]
        backward = [(target, source) for source, target in forward]
        low = lax.ppermute(
            lax.slice_in_dim(block, block.shape[dim] - width, None, axis=dim), axis, forward
        )
        high = lax.ppermute(lax.slice_in_dim(block, 0, width, axis=dim), axis, backward)
        block = jnp.concatenate([low, block, high], axis=dim)
    return block


def advect(field, velocity):
    padded = extended(field, (("row", 1), ("col", 2)), 1)
    along_x = padded[:, 2:, 1:-1] - padded[:, :-2, 1:-1]
    along_y = padded[:, 1:-1, 2:] - padded[:, 1:-1, :-2]
    return -0.5 * (
        velocity[:, 0][:, None, None] * along_x + velocity[:, 1][:, None, None] * along_y
    )


def blockmul(matrix, field):
    return jnp.sum(matrix * field[None], axis=1)


def least_squares(hessen, beta):
    width = hessen.shape[1]
    rotated = jnp.zeros((width + 1,), jnp.float32).at[0].set(beta)
    upper = hessen
    for index in range(width):
        first = upper[index, index]
        second = upper[index + 1, index]
        radius = jnp.sqrt(first * first + second * second)
        cosine = first / radius
        sine = second / radius
        row_top = cosine * upper[index] + sine * upper[index + 1]
        row_low = -sine * upper[index] + cosine * upper[index + 1]
        upper = upper.at[index].set(row_top).at[index + 1].set(row_low)
        g_top = cosine * rotated[index] + sine * rotated[index + 1]
        g_low = -sine * rotated[index] + cosine * rotated[index + 1]
        rotated = rotated.at[index].set(g_top).at[index + 1].set(g_low)
    coef = jnp.zeros((width,), jnp.float32)
    for index in reversed(range(width)):
        partial_sum = jnp.sum(upper[index, index + 1 : width] * coef[index + 1 : width])
        coef = coef.at[index].set((rotated[index] - partial_sum) / upper[index, index])
    return (coef, jnp.abs(rotated[width]))


def body(state, history, rates, quadratic, velocity, precond):
    forcing = advect(state, velocity) + blockmul(rates, state) - quadratic * state * state
    rhs = -(state - history - step_gamma * forcing)
    beta = jnp.sqrt(lax.psum(jnp.sum(rhs * rhs), ("row", "col")) + tiny_eps)
    basis = [rhs / beta]
    kept = []
    hessen = jnp.zeros((KRYLOV + 1, KRYLOV), jnp.float32)
    for index in range(KRYLOV):
        direct = blockmul(precond, basis[index])
        kept.append(direct)
        jac = advect(direct, velocity) + blockmul(rates, direct) - 2.0 * quadratic * state * direct
        vector = direct - step_gamma * jac
        stacked = jnp.stack(basis)
        local_dots = jnp.sum(stacked * vector[None], axis=(1, 2, 3))
        dots, before = lax.psum((local_dots, jnp.sum(vector * vector)), ("row", "col"))
        vector = vector - jnp.sum(dots[:, None, None, None] * stacked, axis=0)
        squared = before - jnp.sum(dots * dots)
        size_new = jnp.sqrt(squared + tiny_eps)
        hessen = hessen.at[: index + 1, index].set(dots).at[index + 1, index].set(size_new)
        basis.append(vector / size_new)
    coef, lin_norm = least_squares(hessen, beta)
    combined = jnp.sum(coef[:, None, None, None] * jnp.stack(basis[:KRYLOV]), axis=0)
    correction = blockmul(precond, combined)
    return (state + correction, jnp.reshape(lin_norm, (1,)))


def solution(mesh):
    placed = (
        P(None, ("parts", "row"), "col"),
        P(None, ("parts", "row"), "col"),
        P(None, None, ("parts", "row"), "col"),
        P(None, ("parts", "row"), "col"),
        P(),
        P(None, None, ("parts", "row"), "col"),
    )
    return jax.shard_map(
        body,
        mesh=mesh,
        in_specs=placed,
        out_specs=(P(None, ("parts", "row"), "col"), P("parts")),
        check_vma=False,
    )
```

profile of v0, /device:TPU:0, one launch (start us, length us, event | category | flops | bytes accessed | tf_op | source)
XLA Modules:
  0.0 279.6 jit_solution(16215169505555502827)
XLA Ops:
  0.6 0.8 fusion.64
  1.4 1.3 collective-permute-start
  2.7 5.6 %collective-permute-start.1 = (f32[10,1,128]{2,1,0:T(1,128)S(1)}, f32[10,1,128]{2,1,0:T(1,128)S(1)}, u32[]{:S(2)}, u32[]{:S(2)}) collective-permute-start(f32[10,1,128]{2,1,0:T(1,128)S(1)} %get-tuple-element.388), channel_id=1, source_target_pairs={{0,4},{4,8},{8,12},{1,5},{5,9},{9,13},{2,6},{6,10},{10,14},{3,7},{... | collective-permute-start | bytes 15368 | tf_op jit(solution)/shard_map/ppermute | solution.py:16
  8.4 1.3 multiply_reduce_fusion.9
  9.7 0.6 fusion.71
  10.3 0.7 and_reduce_fusion.1
  11.0 0.7 and_reduce_fusion
  11.8 0.6 fusion.70
  12.5 1.3 collective-permute-start.2
  13.8 3.0 %collective-permute-start.3 = (f32[10,18,1]{2,1,0:T(8,128)S(1)}, f32[10,18,1]{2,1,0:T(8,128)S(1)}, u32[]{:S(2)}, u32[]{:S(2)}) collective-permute-start(f32[10,18,1]{2,1,0:T(8,128)S(1)} %get-tuple-element.379), channel_id=1, source_target_pairs={{0,1},{1,2},{2,3},{4,5},{5,6},{6,7},{8,9},{9,10},{10,11},{12,13},{... | collective-permute-start | bytes 2168 | tf_op jit(solution)/shard_map/ppermute | solution.py:16
  16.9 0.9 collective-permute-done.3
  17.8 0.8 multiply_reduce_fusion.21
  18.6 33.0 %psum.63 = f32[]{:T(128)} all-reduce(f32[]{:T(128)} %get-tuple-element.368), channel_id=1, replica_groups=mesh['parts'=2,'row'=4,'col'=4] {'row','col'}, use_global_device_ids=true, to_apply=%region_2.0 | all-reduce | flops 1 | bytes 8 | tf_op jit(solution)/shard_map/psum | solution.py:63
  52.4 1.4 collective-permute-start.4
  53.9 4.5 %collective-permute-start.5 = (f32[10,1,128]{2,1,0:T(1,128)S(1)}, f32[10,1,128]{2,1,0:T(1,128)S(1)}, u32[]{:S(2)}, u32[]{:S(2)}) collective-permute-start(f32[10,1,128]{2,1,0:T(1,128)S(1)} %get-tuple-element.386), channel_id=1, source_target_pairs={{0,4},{4,8},{8,12},{1,5},{5,9},{9,13},{2,6},{6,10},{10,14},{3,7},{... | collective-permute-start | bytes 15368 | tf_op jit(solution)/shard_map/ppermute | solution.py:16
  58.4 0.6 fusion.69
  59.0 0.6 compare_reduce_fusion
  59.9 1.3 collective-permute-start.6
  61.2 3.0 %collective-permute-start.7 = (f32[10,18,1]{2,1,0:T(8,128)S(1)}, f32[10,18,1]{2,1,0:T(8,128)S(1)}, u32[]{:S(2)}, u32[]{:S(2)}) collective-permute-start(f32[10,18,1]{2,1,0:T(8,128)S(1)} %get-tuple-element.377), channel_id=1, source_target_pairs={{0,1},{1,2},{2,3},{4,5},{5,6},{6,7},{8,9},{9,10},{10,11},{12,13},{... | collective-permute-start | bytes 2168 | tf_op jit(solution)/shard_map/ppermute | solution.py:16
  64.3 0.9 collective-permute-done.7
  65.2 0.8 multiply_reduce_fusion.20
  66.0 31.1 %all-reduce.6 = (f32[]{:T(128)}, f32[1]{0:T(128)}) all-reduce(f32[]{:T(128)} %get-tuple-element.351, f32[1]{0:T(128)} %bitcast.2), channel_id=1, replica_groups=mesh['parts'=2,'row'=4,'col'=4] {'row','col'}, use_global_device_ids=true, to_apply=%region_8.0 | all-reduce | flops 2 | bytes 16 | tf_op jit(solution)/shard_map/psum | solution.py:74
  99.1 0.7 subtract_divide_fusion.2
  99.8 1.3 collective-permute-start.8
  101.1 4.5 %collective-permute-start.9 = (f32[10,1,128]{2,1,0:T(1,128)S(1)}, f32[10,1,128]{2,1,0:T(1,128)S(1)}, u32[]{:S(2)}, u32[]{:S(2)}) collective-permute-start(f32[10,1,128]{2,1,0:T(1,128)S(1)} %get-tuple-element.384), channel_id=1, source_target_pairs={{0,4},{4,8},{8,12},{1,5},{5,9},{9,13},{2,6},{6,10},{10,14},{3,7},{... | collective-permute-start | bytes 15368 | tf_op jit(solution)/shard_map/ppermute | solution.py:16
  105.7 1.3 collective-permute-done.9
  107.1 1.3 collective-permute-start.10
  108.4 3.0 %collective-permute-start.11 = (f32[10,18,1]{2,1,0:T(8,128)S(1)}, f32[10,18,1]{2,1,0:T(8,128)S(1)}, u32[]{:S(2)}, u32[]{:S(2)}) collective-permute-start(f32[10,18,1]{2,1,0:T(8,128)S(1)} %get-tuple-element.375), channel_id=1, source_target_pairs={{0,1},{1,2},{2,3},{4,5},{5,6},{6,7},{8,9},{9,10},{10,11},{12,13},{... | collective-permute-start | bytes 2168 | tf_op jit(solution)/shard_map/ppermute | solution.py:16
  111.6 0.7 scatter.56
  112.4 0.8 multiply_reduce_fusion.18
  113.3 31.0 %all-reduce.5 = (f32[2]{0:T(128)S(1)}, f32[]{:T(128)}) all-reduce(f32[2]{0:T(128)S(1)} %multiply_reduce_fusion.15, f32[]{:T(128)} %get-tuple-element.364), channel_id=1, replica_groups=mesh['parts'=2,'row'=4,'col'=4] {'row','col'}, use_global_device_ids=true, to_apply=%region_13.0 | all-reduce | flops 3 | bytes 24 | tf_op jit(solution)/shard_map/psum | solution.py:74
  144.4 0.7 multiply_reduce_fusion.26
  146.6 1.3 collective-permute-start.12
  147.9 4.5 %collective-permute-start.13 = (f32[10,1,128]{2,1,0:T(1,128)S(1)}, f32[10,1,128]{2,1,0:T(1,128)S(1)}, u32[]{:S(2)}, u32[]{:S(2)}) collective-permute-start(f32[10,1,128]{2,1,0:T(1,128)S(1)} %get-tuple-element.382), channel_id=1, source_target_pairs={{0,4},{4,8},{8,12},{1,5},{5,9},{9,13},{2,6},{6,10},{10,14},{3,7},{... | collective-permute-start | bytes 15368 | tf_op jit(solution)/shard_map/ppermute | solution.py:16
  152.4 1.9 broadcast_select_fusion.2
  154.4 1.3 collective-permute-start.14
  155.8 3.0 %collective-permute-start.15 = (f32[10,18,1]{2,1,0:T(8,128)S(1)}, f32[10,18,1]{2,1,0:T(8,128)S(1)}, u32[]{:S(2)}, u32[]{:S(2)}) collective-permute-start(f32[10,18,1]{2,1,0:T(8,128)S(1)} %get-tuple-element.373), channel_id=1, source_target_pairs={{0,1},{1,2},{2,3},{4,5},{5,6},{6,7},{8,9},{9,10},{10,11},{12,13},{... | collective-permute-start | bytes 2168 | tf_op jit(solution)/shard_map/ppermute | solution.py:16
  158.9 1.4 scatter.60
  160.4 0.8 multiply_reduce_fusion.17
  161.3 30.3 %all-reduce.4 = (f32[3]{0:T(128)S(1)}, f32[]{:T(128)}) all-reduce(f32[3]{0:T(128)S(1)} %multiply_reduce_fusion.13, f32[]{:T(128)} %get-tuple-element.362), channel_id=1, replica_groups=mesh['parts'=2,'row'=4,'col'=4] {'row','col'}, use_global_device_ids=true, to_apply=%region_22.0 | all-reduce | flops 4 | bytes 32 | tf_op jit(solution)/shard_map/psum | solution.py:74
  191.7 0.6 multiply_reduce_fusion.25
  193.7 1.3 collective-permute-start.16
  195.0 4.5 %collective-permute-start.17 = (f32[10,1,128]{2,1,0:T(1,128)S(1)}, f32[10,1,128]{2,1,0:T(1,128)S(1)}, u32[]{:S(2)}, u32[]{:S(2)}) collective-permute-start(f32[10,1,128]{2,1,0:T(1,128)S(1)} %get-tuple-element.380), channel_id=1, source_target_pairs={{0,4},{4,8},{8,12},{1,5},{5,9},{9,13},{2,6},{6,10},{10,14},{3,7},{... | collective-permute-start | bytes 15368 | tf_op jit(solution)/shard_map/ppermute | solution.py:16
  199.6 1.9 broadcast_select_fusion.1
  201.6 1.3 collective-permute-start.18
  202.9 3.0 %collective-permute-start.19 = (f32[10,18,1]{2,1,0:T(8,128)S(1)}, f32[10,18,1]{2,1,0:T(8,128)S(1)}, u32[]{:S(2)}, u32[]{:S(2)}) collective-permute-start(f32[10,18,1]{2,1,0:T(8,128)S(1)} %get-tuple-element.371), channel_id=1, source_target_pairs={{0,1},{1,2},{2,3},{4,5},{5,6},{6,7},{8,9},{9,10},{10,11},{12,13},{... | collective-permute-start | bytes 2168 | tf_op jit(solution)/shard_map/ppermute | solution.py:16
  206.0 1.4 scatter.64
  207.6 0.8 multiply_reduce_fusion.16
  208.5 30.7 %all-reduce.3 = (f32[4]{0:T(128)S(1)}, f32[]{:T(128)}) all-reduce(f32[4]{0:T(128)S(1)} %multiply_reduce_fusion.11, f32[]{:T(128)} %get-tuple-element.360), channel_id=1, replica_groups=mesh['parts'=2,'row'=4,'col'=4] {'row','col'}, use_global_device_ids=true, to_apply=%region_31.0 | all-reduce | flops 5 | bytes 40 | tf_op jit(solution)/shard_map/psum | solution.py:74
  239.2 0.7 multiply_reduce_fusion.24
  241.1 2.0 broadcast_select_fusion
  243.1 1.3 scatter.66
  244.6 0.7 fusion.67
  249.4 0.7 fusion.66
  254.4 0.5 slice.739
  259.0 0.5 slice.741
  263.5 0.6 slice.745
  265.4 0.6 fusion.68
  268.6 0.5 slice.756
  269.8 0.5 slice.750
  270.3 0.6 fusion.65
  272.9 0.7 multiply_reduce_fusion.23
  275.0 0.7 multiply_reduce_fusion.22
  277.8 0.6 add.240
  (91 shorter events, 4.4 us)
Async XLA Ops:
  1.4 10.9 %collective-permute-start = (f32[10,1,128]{2,1,0:T(1,128)S(1)}, f32[10,1,128]{2,1,0:T(1,128)S(1)}, u32[]{:S(2)}, u32[]{:S(2)}) collective-permute-start(f32[10,1,128]{2,1,0:T(1,128)S(1)} %get-tuple-element.389), channel_id=1, source_target_pairs={{4,0},{8,4},{12,8},{5,1},{9,5},{13,9},{6,2},{10,6},{14,10},{7,3},{... | collective-permute-start | bytes 15368 | tf_op jit(solution)/shard_map/ppermute | solution.py:19
  2.7 5.6 %copy-start.5 = (f32[10,2]{0,1:T(2,128)S(1)}, f32[10,2]{0,1:T(2,128)}, u32[]{:S(2)}) copy-start(f32[10,2]{0,1:T(2,128)} %param.68) | copy-start | bytes 244
  2.7 9.6 %collective-permute-start.1 = (f32[10,1,128]{2,1,0:T(1,128)S(1)}, f32[10,1,128]{2,1,0:T(1,128)S(1)}, u32[]{:S(2)}, u32[]{:S(2)}) collective-permute-start(f32[10,1,128]{2,1,0:T(1,128)S(1)} %get-tuple-element.388), channel_id=1, source_target_pairs={{0,4},{4,8},{8,12},{1,5},{5,9},{9,13},{2,6},{6,10},{10,14},{3,7},{... | collective-permute-start | bytes 15368 | tf_op jit(solution)/shard_map/ppermute | solution.py:16
  8.4 2.0 copy-start.6
  8.4 2.7 copy-start.7
  8.4 4.0 %copy-start.2 = (f32[10,16,128]{2,1,0:T(8,128)S(1)}, f32[10,16,128]{2,1,0:T(8,128)}, u32[]{:S(2)}) copy-start(f32[10,16,128]{2,1,0:T(8,128)} %param.64) | copy-start | bytes 245764
  8.4 9.4 %copy-start.3 = (f32[10,16,128]{2,1,0:T(8,128)S(1)}, f32[10,16,128]{2,1,0:T(8,128)}, u32[]{:S(2)}) copy-start(f32[10,16,128]{2,1,0:T(8,128)} %param.67) | copy-start | bytes 245764
  8.4 9.4 %copy-start.4 = (f32[10,16,128]{2,1,0:T(8,128)S(1)}, f32[10,16,128]{2,1,0:T(8,128)}, u32[]{:S(2)}) copy-start(f32[10,16,128]{2,1,0:T(8,128)} %param.65) | copy-start | bytes 245764
  9.7 42.6 %copy-start.1 = (f32[10,10,16,128]{3,2,1,0:T(8,128)S(1)}, f32[10,10,16,128]{3,2,1,0:T(8,128)}, u32[]{:S(2)}) copy-start(f32[10,10,16,128]{3,2,1,0:T(8,128)} %param.69) | copy-start | bytes 2457604
  12.5 4.4 %collective-permute-start.2 = (f32[10,18,1]{2,1,0:T(8,128)S(1)}, f32[10,18,1]{2,1,0:T(8,128)S(1)}, u32[]{:S(2)}, u32[]{:S(2)}) collective-permute-start(f32[10,18,1]{2,1,0:T(8,128)S(1)} %get-tuple-element.378), channel_id=1, source_target_pairs={{1,0},{2,1},{3,2},{5,4},{6,5},{7,6},{9,8},{10,9},{11,10},{13,12},{... | collective-permute-start | bytes 2168 | tf_op jit(solution)/shard_map/ppermute | solution.py:19
  13.8 4.0 %collective-permute-start.3 = (f32[10,18,1]{2,1,0:T(8,128)S(1)}, f32[10,18,1]{2,1,0:T(8,128)S(1)}, u32[]{:S(2)}, u32[]{:S(2)}) collective-permute-start(f32[10,18,1]{2,1,0:T(8,128)S(1)} %get-tuple-element.379), channel_id=1, source_target_pairs={{0,1},{1,2},{2,3},{4,5},{5,6},{6,7},{8,9},{9,10},{10,11},{12,13},{... | collective-permute-start | bytes 2168 | tf_op jit(solution)/shard_map/ppermute | solution.py:16
  52.3 11.9 %copy-start = (f32[10,10,16,128]{3,2,1,0:T(8,128)S(1)}, f32[10,10,16,128]{3,2,1,0:T(8,128)}, u32[]{:S(2)}) copy-start(f32[10,10,16,128]{3,2,1,0:T(8,128)} %param.66) | copy-start | bytes 2457604
  52.4 7.2 %collective-permute-start.4 = (f32[10,1,128]{2,1,0:T(1,128)S(1)}, f32[10,1,128]{2,1,0:T(1,128)S(1)}, u32[]{:S(2)}, u32[]{:S(2)}) collective-permute-start(f32[10,1,128]{2,1,0:T(1,128)S(1)} %get-tuple-element.387), channel_id=1, source_target_pairs={{4,0},{8,4},{12,8},{5,1},{9,5},{13,9},{6,2},{10,6},{14,10},{7,3},{... | collective-permute-start | bytes 15368 | tf_op jit(solution)/shard_map/ppermute | solution.py:19
  53.9 5.9 %collective-permute-start.5 = (f32[10,1,128]{2,1,0:T(1,128)S(1)}, f32[10,1,128]{2,1,0:T(1,128)S(1)}, u32[]{:S(2)}, u32[]{:S(2)}) collective-permute-start(f32[10,1,128]{2,1,0:T(1,128)S(1)} %get-tuple-element.386), channel_id=1, source_target_pairs={{0,4},{4,8},{8,12},{1,5},{5,9},{9,13},{2,6},{6,10},{10,14},{3,7},{... | collective-permute-start | bytes 15368 | tf_op jit(solution)/shard_map/ppermute | solution.py:16
  59.9 4.4 %collective-permute-start.6 = (f32[10,18,1]{2,1,0:T(8,128)S(1)}, f32[10,18,1]{2,1,0:T(8,128)S(1)}, u32[]{:S(2)}, u32[]{:S(2)}) collective-permute-start(f32[10,18,1]{2,1,0:T(8,128)S(1)} %get-tuple-element.376), channel_id=1, source_target_pairs={{1,0},{2,1},{3,2},{5,4},{6,5},{7,6},{9,8},{10,9},{11,10},{13,12},{... | collective-permute-start | bytes 2168 | tf_op jit(solution)/shard_map/ppermute | solution.py:19
  61.2 4.0 %collective-permute-start.7 = (f32[10,18,1]{2,1,0:T(8,128)S(1)}, f32[10,18,1]{2,1,0:T(8,128)S(1)}, u32[]{:S(2)}, u32[]{:S(2)}) collective-permute-start(f32[10,18,1]{2,1,0:T(8,128)S(1)} %get-tuple-element.377), channel_id=1, source_target_pairs={{0,1},{1,2},{2,3},{4,5},{5,6},{6,7},{8,9},{9,10},{10,11},{12,13},{... | collective-permute-start | bytes 2168 | tf_op jit(solution)/shard_map/ppermute | solution.py:16
  99.8 5.9 %collective-permute-start.8 = (f32[10,1,128]{2,1,0:T(1,128)S(1)}, f32[10,1,128]{2,1,0:T(1,128)S(1)}, u32[]{:S(2)}, u32[]{:S(2)}) collective-permute-start(f32[10,1,128]{2,1,0:T(1,128)S(1)} %get-tuple-element.385), channel_id=1, source_target_pairs={{4,0},{8,4},{12,8},{5,1},{9,5},{13,9},{6,2},{10,6},{14,10},{7,3},{... | collective-permute-start | bytes 15368 | tf_op jit(solution)/shard_map/ppermute | solution.py:19
  101.1 5.9 %collective-permute-start.9 = (f32[10,1,128]{2,1,0:T(1,128)S(1)}, f32[10,1,128]{2,1,0:T(1,128)S(1)}, u32[]{:S(2)}, u32[]{:S(2)}) collective-permute-start(f32[10,1,128]{2,1,0:T(1,128)S(1)} %get-tuple-element.384), channel_id=1, source_target_pairs={{0,4},{4,8},{8,12},{1,5},{5,9},{9,13},{2,6},{6,10},{10,14},{3,7},{... | collective-permute-start | bytes 15368 | tf_op jit(solution)/shard_map/ppermute | solution.py:16
  107.1 5.2 %collective-permute-start.10 = (f32[10,18,1]{2,1,0:T(8,128)S(1)}, f32[10,18,1]{2,1,0:T(8,128)S(1)}, u32[]{:S(2)}, u32[]{:S(2)}) collective-permute-start(f32[10,18,1]{2,1,0:T(8,128)S(1)} %get-tuple-element.374), channel_id=1, source_target_pairs={{1,0},{2,1},{3,2},{5,4},{6,5},{7,6},{9,8},{10,9},{11,10},{13,12},{... | collective-permute-start | bytes 2168 | tf_op jit(solution)/shard_map/ppermute | solution.py:19
  108.4 4.0 %collective-permute-start.11 = (f32[10,18,1]{2,1,0:T(8,128)S(1)}, f32[10,18,1]{2,1,0:T(8,128)S(1)}, u32[]{:S(2)}, u32[]{:S(2)}) collective-permute-start(f32[10,18,1]{2,1,0:T(8,128)S(1)} %get-tuple-element.375), channel_id=1, source_target_pairs={{0,1},{1,2},{2,3},{4,5},{5,6},{6,7},{8,9},{9,10},{10,11},{12,13},{... | collective-permute-start | bytes 2168 | tf_op jit(solution)/shard_map/ppermute | solution.py:16
  146.6 7.7 %collective-permute-start.12 = (f32[10,1,128]{2,1,0:T(1,128)S(1)}, f32[10,1,128]{2,1,0:T(1,128)S(1)}, u32[]{:S(2)}, u32[]{:S(2)}) collective-permute-start(f32[10,1,128]{2,1,0:T(1,128)S(1)} %get-tuple-element.383), channel_id=1, source_target_pairs={{4,0},{8,4},{12,8},{5,1},{9,5},{13,9},{6,2},{10,6},{14,10},{7,3},{... | collective-permute-start | bytes 15368 | tf_op jit(solution)/shard_map/ppermute | solution.py:19
  147.9 6.4 %collective-permute-start.13 = (f32[10,1,128]{2,1,0:T(1,128)S(1)}, f32[10,1,128]{2,1,0:T(1,128)S(1)}, u32[]{:S(2)}, u32[]{:S(2)}) collective-permute-start(f32[10,1,128]{2,1,0:T(1,128)S(1)} %get-tuple-element.382), channel_id=1, source_target_pairs={{0,4},{4,8},{8,12},{1,5},{5,9},{9,13},{2,6},{6,10},{10,14},{3,7},{... | collective-permute-start | bytes 15368 | tf_op jit(solution)/shard_map/ppermute | solution.py:16
  154.4 6.0 %collective-permute-start.14 = (f32[10,18,1]{2,1,0:T(8,128)S(1)}, f32[10,18,1]{2,1,0:T(8,128)S(1)}, u32[]{:S(2)}, u32[]{:S(2)}) collective-permute-start(f32[10,18,1]{2,1,0:T(8,128)S(1)} %get-tuple-element.372), channel_id=1, source_target_pairs={{1,0},{2,1},{3,2},{5,4},{6,5},{7,6},{9,8},{10,9},{11,10},{13,12},{... | collective-permute-start | bytes 2168 | tf_op jit(solution)/shard_map/ppermute | solution.py:19
  155.8 4.7 %collective-permute-start.15 = (f32[10,18,1]{2,1,0:T(8,128)S(1)}, f32[10,18,1]{2,1,0:T(8,128)S(1)}, u32[]{:S(2)}, u32[]{:S(2)}) collective-permute-start(f32[10,18,1]{2,1,0:T(8,128)S(1)} %get-tuple-element.373), channel_id=1, source_target_pairs={{0,1},{1,2},{2,3},{4,5},{5,6},{6,7},{8,9},{9,10},{10,11},{12,13},{... | collective-permute-start | bytes 2168 | tf_op jit(solution)/shard_map/ppermute | solution.py:16
  193.7 7.8 %collective-permute-start.16 = (f32[10,1,128]{2,1,0:T(1,128)S(1)}, f32[10,1,128]{2,1,0:T(1,128)S(1)}, u32[]{:S(2)}, u32[]{:S(2)}) collective-permute-start(f32[10,1,128]{2,1,0:T(1,128)S(1)} %get-tuple-element.381), channel_id=1, source_target_pairs={{4,0},{8,4},{12,8},{5,1},{9,5},{13,9},{6,2},{10,6},{14,10},{7,3},{... | collective-permute-start | bytes 15368 | tf_op jit(solution)/shard_map/ppermute | solution.py:19
  195.0 6.5 %collective-permute-start.17 = (f32[10,1,128]{2,1,0:T(1,128)S(1)}, f32[10,1,128]{2,1,0:T(1,128)S(1)}, u32[]{:S(2)}, u32[]{:S(2)}) collective-permute-start(f32[10,1,128]{2,1,0:T(1,128)S(1)} %get-tuple-element.380), channel_id=1, source_target_pairs={{0,4},{4,8},{8,12},{1,5},{5,9},{9,13},{2,6},{6,10},{10,14},{3,7},{... | collective-permute-start | bytes 15368 | tf_op jit(solution)/shard_map/ppermute | solution.py:16
  201.6 5.9 %collective-permute-start.18 = (f32[10,18,1]{2,1,0:T(8,128)S(1)}, f32[10,18,1]{2,1,0:T(8,128)S(1)}, u32[]{:S(2)}, u32[]{:S(2)}) collective-permute-start(f32[10,18,1]{2,1,0:T(8,128)S(1)} %get-tuple-element.370), channel_id=1, source_target_pairs={{1,0},{2,1},{3,2},{5,4},{6,5},{7,6},{9,8},{10,9},{11,10},{13,12},{... | collective-permute-start | bytes 2168 | tf_op jit(solution)/shard_map/ppermute | solution.py:19
  202.9 4.6 %collective-permute-start.19 = (f32[10,18,1]{2,1,0:T(8,128)S(1)}, f32[10,18,1]{2,1,0:T(8,128)S(1)}, u32[]{:S(2)}, u32[]{:S(2)}) collective-permute-start(f32[10,18,1]{2,1,0:T(8,128)S(1)} %get-tuple-element.371), channel_id=1, source_target_pairs={{0,1},{1,2},{2,3},{4,5},{5,6},{6,7},{8,9},{9,10},{10,11},{12,13},{... | collective-permute-start | bytes 2168 | tf_op jit(solution)/shard_map/ppermute | solution.py:16
where the time goes:
time: 281 us; the launch traced here: 280 us
  blocking collectives  156 us (56%)
  starting transfers between devices  52 us (19%)
  between operations  33.8 us (12%)
  other arithmetic  19.4 us (7%)
  local copies, waits for them, and re-layouts  15 us (5%)
  waiting for transfers between devices  3.3 us (1%)
    psum x4, blocking collectives, body(): lax.psum((local_dots, jnp.sum(vector * vector)), ('row', 'col'))  123 us
    ppermute x10, starting transfers between devices, extended(): lax.ppermute(lax.slice_in_dim(block, block.shape[dim] - width, None, axis...  39 us
    psum x1, blocking collectives, body(): beta = jnp.sqrt(lax.psum(jnp.sum(rhs * rhs), ('row', 'col')) + tiny_eps)  33 us
    ppermute x10, starting transfers between devices, extended(): lax.ppermute(lax.slice_in_dim(block, 0, width, axis=dim), axis, backward)  13 us
    another operation x8, other arithmetic  7.82 us
  transfers between devices with their start and end apart: 20, of which 5 were waited for; matrix products, arithmetic and copies ran while one was open for 5% of the time, Pallas kernels for 0%

commit v1 on v0

--- a/solution.py
+++ b/solution.py
@@ -1,11 +1,22 @@
+import functools
 import jax
 import jax.numpy as jnp
 from jax import lax
 from jax.sharding import PartitionSpec as P
+from jax.lax import psum
 
 KRYLOV = 4
 step_gamma = 0.4
 tiny_eps = 1e-12
+
+
+def guide_modes(array_here, mesh_dim, a_name):
+    found_now = psum(array_here, mesh_dim)
+    val = psum(found_now, a_name)
+    return val
+
+
+hold_series_all = functools.partial(guide_modes, mesh_dim="col", a_name="row")
 
 
 def extended(block, sides, width):
@@ -71,7 +82,7 @@
         vector = direct - step_gamma * jac
         stacked = jnp.stack(basis)
         local_dots = jnp.sum(stacked * vector[None], axis=(1, 2, 3))
-        dots, before = lax.psum((local_dots, jnp.sum(vector * vector)), ("row", "col"))
+        dots, before = hold_series_all((local_dots, jnp.sum(vector * vector)))
         vector = vector - jnp.sum(dots[:, None, None, None] * stacked, axis=0)
         squared = before - jnp.sum(dots * dots)
         size_new = jnp.sqrt(squared + tiny_eps)

time: 281 us -> 236 us (0.84)
  blocking collectives: 156 us -> 111 us
    psum x4 -> x8, blocking collectives: 123 us -> 77.6 us  [the longest x4 43.9 us: guide_modes(): val = psum(found_now, a_name)]
  transfers between devices with their start and end apart: 20 -> 20, of which waited for: 5 -> 5; matrix products, arithmetic and copies ran while one was open for 5% -> 6% of each run, Pallas kernels for 0% -> 0%
where the time goes in v1:
time: 236 us; the launch traced here: 234 us
  blocking collectives  111 us (47%)
  starting transfers between devices  52 us (22%)
  between operations  33.7 us (14%)
  other arithmetic  19.4 us (8%)
  local copies, waits for them, and re-layouts  15 us (6%)
  waiting for transfers between devices  3.3 us (1%)
    psum x4, blocking collectives, guide_modes(): val = psum(found_now, a_name)  43.9 us
    ppermute x10, starting transfers between devices, extended(): lax.ppermute(lax.slice_in_dim(block, block.shape[dim] - width, None, axis...  39 us
    psum x4, blocking collectives, guide_modes(): found_now = psum(array_here, mesh_dim)  33.7 us
    psum x1, blocking collectives, body(): beta = jnp.sqrt(lax.psum(jnp.sum(rhs * rhs), ('row', 'col')) + tiny_eps)  33 us
    ppermute x10, starting transfers between devices, extended(): lax.ppermute(lax.slice_in_dim(block, 0, width, axis=dim), axis, backward)  13 us
    another operation x8, other arithmetic  7.82 us
    scatter x8, local copies, waits for them, and re-layouts, body(): hessen.at[:index + 1, index].set(dots).at[index + 1, index].set(size_new)  5.25 us
  transfers between devices with their start and end apart: 20, of which 5 were waited for; matrix products, arithmetic and copies ran while one was open for 6% of the time, Pallas kernels for 0%

profile of v1, /device:TPU:0, one launch (start us, length us, event | category | flops | bytes accessed | tf_op | source)
XLA Modules:
  0.0 234.1 jit_solution(16033318331616442864)
XLA Ops:
  0.6 0.8 fusion.64
  1.4 1.3 collective-permute-start
  2.7 5.6 %collective-permute-start.1 = (f32[10,1,128]{2,1,0:T(1,128)S(1)}, f32[10,1,128]{2,1,0:T(1,128)S(1)}, u32[]{:S(2)}, u32[]{:S(2)}) collective-permute-start(f32[10,1,128]{2,1,0:T(1,128)S(1)} %get-tuple-element.396), channel_id=1, source_target_pairs={{0,4},{4,8},{8,12},{1,5},{5,9},{9,13},{2,6},{6,10},{10,14},{3,7},{... | collective-permute-start | bytes 15368 | tf_op jit(solution)/shard_map/ppermute | solution.py:27
  8.4 1.3 multiply_reduce_fusion.9
  9.7 0.6 fusion.71
  10.3 0.7 and_reduce_fusion.1
  11.0 0.7 and_reduce_fusion
  11.8 0.6 fusion.70
  12.5 1.3 collective-permute-start.2
  13.8 3.0 %collective-permute-start.3 = (f32[10,18,1]{2,1,0:T(8,128)S(1)}, f32[10,18,1]{2,1,0:T(8,128)S(1)}, u32[]{:S(2)}, u32[]{:S(2)}) collective-permute-start(f32[10,18,1]{2,1,0:T(8,128)S(1)} %get-tuple-element.387), channel_id=1, source_target_pairs={{0,1},{1,2},{2,3},{4,5},{5,6},{6,7},{8,9},{9,10},{10,11},{12,13},{... | collective-permute-start | bytes 2168 | tf_op jit(solution)/shard_map/ppermute | solution.py:27
  16.9 0.9 collective-permute-done.3
  17.8 0.8 multiply_reduce_fusion.21
  18.6 33.0 %psum.119 = f32[]{:T(128)} all-reduce(f32[]{:T(128)} %get-tuple-element.376), channel_id=1, replica_groups=mesh['parts'=2,'row'=4,'col'=4] {'row','col'}, use_global_device_ids=true, to_apply=%region_2.0 | all-reduce | flops 1 | bytes 8 | tf_op jit(solution)/shard_map/psum | solution.py:74
  52.4 1.4 collective-permute-start.4
  53.9 4.5 %collective-permute-start.5 = (f32[10,1,128]{2,1,0:T(1,128)S(1)}, f32[10,1,128]{2,1,0:T(1,128)S(1)}, u32[]{:S(2)}, u32[]{:S(2)}) collective-permute-start(f32[10,1,128]{2,1,0:T(1,128)S(1)} %get-tuple-element.394), channel_id=1, source_target_pairs={{0,4},{4,8},{8,12},{1,5},{5,9},{9,13},{2,6},{6,10},{10,14},{3,7},{... | collective-permute-start | bytes 15368 | tf_op jit(solution)/shard_map/ppermute | solution.py:27
  58.4 0.6 fusion.69
  59.0 0.6 compare_reduce_fusion
  59.9 1.3 collective-permute-start.6
  61.2 3.0 %collective-permute-start.7 = (f32[10,18,1]{2,1,0:T(8,128)S(1)}, f32[10,18,1]{2,1,0:T(8,128)S(1)}, u32[]{:S(2)}, u32[]{:S(2)}) collective-permute-start(f32[10,18,1]{2,1,0:T(8,128)S(1)} %get-tuple-element.385), channel_id=1, source_target_pairs={{0,1},{1,2},{2,3},{4,5},{5,6},{6,7},{8,9},{9,10},{10,11},{12,13},{... | collective-permute-start | bytes 2168 | tf_op jit(solution)/shard_map/ppermute | solution.py:27
  64.3 0.9 collective-permute-done.7
  65.2 0.8 multiply_reduce_fusion.20
  66.0 7.5 %all-reduce.6 = (f32[]{:T(128)}, f32[1]{0:T(128)}) all-reduce(f32[]{:T(128)} %get-tuple-element.351, f32[1]{0:T(128)} %bitcast.2), channel_id=1, replica_groups=mesh['parts'=2,'row'=4,'col'=4] {'col'}, use_global_device_ids=true, to_apply=%region_9.0 | all-reduce | flops 2 | bytes 16 | tf_op jit(solution)/shard_map/psum | solution.py:14
  73.4 11.3 %all-reduce.10 = (f32[]{:T(128)}, f32[1]{0:T(128)}) all-reduce(f32[]{:T(128)} %get-tuple-element.358, f32[1]{0:T(128)} %get-tuple-element.359), channel_id=1, replica_groups=mesh['parts'=2,'row'=4,'col'=4] {'row'}, use_global_device_ids=true, to_apply=%region_10.0 | all-reduce | flops 2 | bytes 16 | tf_op jit(solution)/shard_map/psum | solution.py:15
  86.7 0.7 subtract_divide_fusion.2
  87.5 1.3 collective-permute-start.8
  88.8 4.5 %collective-permute-start.9 = (f32[10,1,128]{2,1,0:T(1,128)S(1)}, f32[10,1,128]{2,1,0:T(1,128)S(1)}, u32[]{:S(2)}, u32[]{:S(2)}) collective-permute-start(f32[10,1,128]{2,1,0:T(1,128)S(1)} %get-tuple-element.392), channel_id=1, source_target_pairs={{0,4},{4,8},{8,12},{1,5},{5,9},{9,13},{2,6},{6,10},{10,14},{3,7},{... | collective-permute-start | bytes 15368 | tf_op jit(solution)/shard_map/ppermute | solution.py:27
  93.4 1.3 collective-permute-done.9
  94.8 1.3 collective-permute-start.10
  96.1 3.0 %collective-permute-start.11 = (f32[10,18,1]{2,1,0:T(8,128)S(1)}, f32[10,18,1]{2,1,0:T(8,128)S(1)}, u32[]{:S(2)}, u32[]{:S(2)}) collective-permute-start(f32[10,18,1]{2,1,0:T(8,128)S(1)} %get-tuple-element.383), channel_id=1, source_target_pairs={{0,1},{1,2},{2,3},{4,5},{5,6},{6,7},{8,9},{9,10},{10,11},{12,13},{... | collective-permute-start | bytes 2168 | tf_op jit(solution)/shard_map/ppermute | solution.py:27
  99.2 0.7 scatter.56
  100.1 0.8 multiply_reduce_fusion.18
  101.0 9.2 %all-reduce.5 = (f32[2]{0:T(128)S(1)}, f32[]{:T(128)}) all-reduce(f32[2]{0:T(128)S(1)} %multiply_reduce_fusion.15, f32[]{:T(128)} %get-tuple-element.372), channel_id=1, replica_groups=mesh['parts'=2,'row'=4,'col'=4] {'col'}, use_global_device_ids=true, to_apply=%region_15.0 | all-reduce | flops 3 | bytes 24 | tf_op jit(solution)/shard_map/psum | solution.py:14
  110.2 11.2 %all-reduce.9 = (f32[2]{0:T(128)S(1)}, f32[]{:T(128)}) all-reduce(f32[2]{0:T(128)S(1)} %get-tuple-element.356, f32[]{:T(128)} %get-tuple-element.357), channel_id=1, replica_groups=mesh['parts'=2,'row'=4,'col'=4] {'row'}, use_global_device_ids=true, to_apply=%region_16.0 | all-reduce | flops 3 | bytes 24 | tf_op jit(solution)/shard_map/psum | solution.py:15
  121.4 0.7 multiply_reduce_fusion.26
  123.7 1.3 collective-permute-start.12
  125.0 4.5 %collective-permute-start.13 = (f32[10,1,128]{2,1,0:T(1,128)S(1)}, f32[10,1,128]{2,1,0:T(1,128)S(1)}, u32[]{:S(2)}, u32[]{:S(2)}) collective-permute-start(f32[10,1,128]{2,1,0:T(1,128)S(1)} %get-tuple-element.390), channel_id=1, source_target_pairs={{0,4},{4,8},{8,12},{1,5},{5,9},{9,13},{2,6},{6,10},{10,14},{3,7},{... | collective-permute-start | bytes 15368 | tf_op jit(solution)/shard_map/ppermute | solution.py:27
  129.5 1.9 broadcast_select_fusion.2
  131.5 1.3 collective-permute-start.14
  132.8 3.0 %collective-permute-start.15 = (f32[10,18,1]{2,1,0:T(8,128)S(1)}, f32[10,18,1]{2,1,0:T(8,128)S(1)}, u32[]{:S(2)}, u32[]{:S(2)}) collective-permute-start(f32[10,18,1]{2,1,0:T(8,128)S(1)} %get-tuple-element.381), channel_id=1, source_target_pairs={{0,1},{1,2},{2,3},{4,5},{5,6},{6,7},{8,9},{9,10},{10,11},{12,13},{... | collective-permute-start | bytes 2168 | tf_op jit(solution)/shard_map/ppermute | solution.py:27
  135.9 1.4 scatter.60
  137.5 0.8 multiply_reduce_fusion.17
  138.4 8.5 %all-reduce.4 = (f32[3]{0:T(128)S(1)}, f32[]{:T(128)}) all-reduce(f32[3]{0:T(128)S(1)} %multiply_reduce_fusion.13, f32[]{:T(128)} %get-tuple-element.370), channel_id=1, replica_groups=mesh['parts'=2,'row'=4,'col'=4] {'col'}, use_global_device_ids=true, to_apply=%region_26.0 | all-reduce | flops 4 | bytes 32 | tf_op jit(solution)/shard_map/psum | solution.py:14
  146.9 10.7 %all-reduce.8 = (f32[3]{0:T(128)S(1)}, f32[]{:T(128)}) all-reduce(f32[3]{0:T(128)S(1)} %get-tuple-element.354, f32[]{:T(128)} %get-tuple-element.355), channel_id=1, replica_groups=mesh['parts'=2,'row'=4,'col'=4] {'row'}, use_global_device_ids=true, to_apply=%region_27.0 | all-reduce | flops 4 | bytes 32 | tf_op jit(solution)/shard_map/psum | solution.py:15
  157.6 0.6 multiply_reduce_fusion.25
  159.7 1.3 collective-permute-start.16
  161.0 4.5 %collective-permute-start.17 = (f32[10,1,128]{2,1,0:T(1,128)S(1)}, f32[10,1,128]{2,1,0:T(1,128)S(1)}, u32[]{:S(2)}, u32[]{:S(2)}) collective-permute-start(f32[10,1,128]{2,1,0:T(1,128)S(1)} %get-tuple-element.388), channel_id=1, source_target_pairs={{0,4},{4,8},{8,12},{1,5},{5,9},{9,13},{2,6},{6,10},{10,14},{3,7},{... | collective-permute-start | bytes 15368 | tf_op jit(solution)/shard_map/ppermute | solution.py:27
  165.5 1.9 broadcast_select_fusion.1
  167.6 1.3 collective-permute-start.18
  168.9 3.0 %collective-permute-start.19 = (f32[10,18,1]{2,1,0:T(8,128)S(1)}, f32[10,18,1]{2,1,0:T(8,128)S(1)}, u32[]{:S(2)}, u32[]{:S(2)}) collective-permute-start(f32[10,18,1]{2,1,0:T(8,128)S(1)} %get-tuple-element.379), channel_id=1, source_target_pairs={{0,1},{1,2},{2,3},{4,5},{5,6},{6,7},{8,9},{9,10},{10,11},{12,13},{... | collective-permute-start | bytes 2168 | tf_op jit(solution)/shard_map/ppermute | solution.py:27
  172.0 1.4 scatter.64
  173.5 0.8 multiply_reduce_fusion.16
  174.4 8.6 %all-reduce.3 = (f32[4]{0:T(128)S(1)}, f32[]{:T(128)}) all-reduce(f32[4]{0:T(128)S(1)} %multiply_reduce_fusion.11, f32[]{:T(128)} %get-tuple-element.368), channel_id=1, replica_groups=mesh['parts'=2,'row'=4,'col'=4] {'col'}, use_global_device_ids=true, to_apply=%region_37.0 | all-reduce | flops 5 | bytes 40 | tf_op jit(solution)/shard_map/psum | solution.py:14
  183.0 10.6 %all-reduce.7 = (f32[4]{0:T(128)S(1)}, f32[]{:T(128)}) all-reduce(f32[4]{0:T(128)S(1)} %get-tuple-element.352, f32[]{:T(128)} %get-tuple-element.353), channel_id=1, replica_groups=mesh['parts'=2,'row'=4,'col'=4] {'row'}, use_global_device_ids=true, to_apply=%region_38.0 | all-reduce | flops 5 | bytes 40 | tf_op jit(solution)/shard_map/psum | solution.py:15
  193.6 0.7 multiply_reduce_fusion.24
  195.6 2.0 broadcast_select_fusion
  197.6 1.3 scatter.66
  199.1 0.7 fusion.67
  203.9 0.7 fusion.66
  218.0 0.6 slice.745
  219.9 0.6 fusion.68
  224.8 0.6 fusion.65
  227.4 0.7 multiply_reduce_fusion.23
  229.5 0.7 multiply_reduce_fusion.22
  232.3 0.6 add.256
  (95 shorter events, 6.5 us)
Async XLA Ops:
  1.4 10.9 %collective-permute-start = (f32[10,1,128]{2,1,0:T(1,128)S(1)}, f32[10,1,128]{2,1,0:T(1,128)S(1)}, u32[]{:S(2)}, u32[]{:S(2)}) collective-permute-start(f32[10,1,128]{2,1,0:T(1,128)S(1)} %get-tuple-element.397), channel_id=1, source_target_pairs={{4,0},{8,4},{12,8},{5,1},{9,5},{13,9},{6,2},{10,6},{14,10},{7,3},{... | collective-permute-start | bytes 15368 | tf_op jit(solution)/shard_map/ppermute | solution.py:30
  2.7 5.6 %copy-start.5 = (f32[10,2]{0,1:T(2,128)S(1)}, f32[10,2]{0,1:T(2,128)}, u32[]{:S(2)}) copy-start(f32[10,2]{0,1:T(2,128)} %param.68) | copy-start | bytes 244
  2.7 9.6 %collective-permute-start.1 = (f32[10,1,128]{2,1,0:T(1,128)S(1)}, f32[10,1,128]{2,1,0:T(1,128)S(1)}, u32[]{:S(2)}, u32[]{:S(2)}) collective-permute-start(f32[10,1,128]{2,1,0:T(1,128)S(1)} %get-tuple-element.396), channel_id=1, source_target_pairs={{0,4},{4,8},{8,12},{1,5},{5,9},{9,13},{2,6},{6,10},{10,14},{3,7},{... | collective-permute-start | bytes 15368 | tf_op jit(solution)/shard_map/ppermute | solution.py:27
  8.4 2.0 copy-start.6
  8.4 2.7 %copy-start.7 = (s32[2]{0:T(128)S(1)}, s32[2]{0:T(128)}, u32[]{:S(2)}) copy-start(s32[2]{0:T(128)} %constant.663.clone.1) | copy-start | bytes 28
  8.4 4.0 %copy-start.2 = (f32[10,16,128]{2,1,0:T(8,128)S(1)}, f32[10,16,128]{2,1,0:T(8,128)}, u32[]{:S(2)}) copy-start(f32[10,16,128]{2,1,0:T(8,128)} %param.64) | copy-start | bytes 245764
  8.4 9.4 %copy-start.3 = (f32[10,16,128]{2,1,0:T(8,128)S(1)}, f32[10,16,128]{2,1,0:T(8,128)}, u32[]{:S(2)}) copy-start(f32[10,16,128]{2,1,0:T(8,128)} %param.67) | copy-start | bytes 245764
  8.4 9.4 %copy-start.4 = (f32[10,16,128]{2,1,0:T(8,128)S(1)}, f32[10,16,128]{2,1,0:T(8,128)}, u32[]{:S(2)}) copy-start(f32[10,16,128]{2,1,0:T(8,128)} %param.65) | copy-start | bytes 245764
  9.7 42.6 %copy-start.1 = (f32[10,10,16,128]{3,2,1,0:T(8,128)S(1)}, f32[10,10,16,128]{3,2,1,0:T(8,128)}, u32[]{:S(2)}) copy-start(f32[10,10,16,128]{3,2,1,0:T(8,128)} %param.69) | copy-start | bytes 2457604
  12.5 4.4 %collective-permute-start.2 = (f32[10,18,1]{2,1,0:T(8,128)S(1)}, f32[10,18,1]{2,1,0:T(8,128)S(1)}, u32[]{:S(2)}, u32[]{:S(2)}) collective-permute-start(f32[10,18,1]{2,1,0:T(8,128)S(1)} %get-tuple-element.386), channel_id=1, source_target_pairs={{1,0},{2,1},{3,2},{5,4},{6,5},{7,6},{9,8},{10,9},{11,10},{13,12},{... | collective-permute-start | bytes 2168 | tf_op jit(solution)/shard_map/ppermute | solution.py:30
  13.8 4.0 %collective-permute-start.3 = (f32[10,18,1]{2,1,0:T(8,128)S(1)}, f32[10,18,1]{2,1,0:T(8,128)S(1)}, u32[]{:S(2)}, u32[]{:S(2)}) collective-permute-start(f32[10,18,1]{2,1,0:T(8,128)S(1)} %get-tuple-element.387), channel_id=1, source_target_pairs={{0,1},{1,2},{2,3},{4,5},{5,6},{6,7},{8,9},{9,10},{10,11},{12,13},{... | collective-permute-start | bytes 2168 | tf_op jit(solution)/shard_map/ppermute | solution.py:27
  52.3 11.9 %copy-start = (f32[10,10,16,128]{3,2,1,0:T(8,128)S(1)}, f32[10,10,16,128]{3,2,1,0:T(8,128)}, u32[]{:S(2)}) copy-start(f32[10,10,16,128]{3,2,1,0:T(8,128)} %param.66) | copy-start | bytes 2457604
  52.4 7.2 %collective-permute-start.4 = (f32[10,1,128]{2,1,0:T(1,128)S(1)}, f32[10,1,128]{2,1,0:T(1,128)S(1)}, u32[]{:S(2)}, u32[]{:S(2)}) collective-permute-start(f32[10,1,128]{2,1,0:T(1,128)S(1)} %get-tuple-element.395), channel_id=1, source_target_pairs={{4,0},{8,4},{12,8},{5,1},{9,5},{13,9},{6,2},{10,6},{14,10},{7,3},{... | collective-permute-start | bytes 15368 | tf_op jit(solution)/shard_map/ppermute | solution.py:30
  53.9 5.9 %collective-permute-start.5 = (f32[10,1,128]{2,1,0:T(1,128)S(1)}, f32[10,1,128]{2,1,0:T(1,128)S(1)}, u32[]{:S(2)}, u32[]{:S(2)}) collective-permute-start(f32[10,1,128]{2,1,0:T(1,128)S(1)} %get-tuple-element.394), channel_id=1, source_target_pairs={{0,4},{4,8},{8,12},{1,5},{5,9},{9,13},{2,6},{6,10},{10,14},{3,7},{... | collective-permute-start | bytes 15368 | tf_op jit(solution)/shard_map/ppermute | solution.py:27
  59.9 4.4 %collective-permute-start.6 = (f32[10,18,1]{2,1,0:T(8,128)S(1)}, f32[10,18,1]{2,1,0:T(8,128)S(1)}, u32[]{:S(2)}, u32[]{:S(2)}) collective-permute-start(f32[10,18,1]{2,1,0:T(8,128)S(1)} %get-tuple-element.384), channel_id=1, source_target_pairs={{1,0},{2,1},{3,2},{5,4},{6,5},{7,6},{9,8},{10,9},{11,10},{13,12},{... | collective-permute-start | bytes 2168 | tf_op jit(solution)/shard_map/ppermute | solution.py:30
  61.2 4.0 %collective-permute-start.7 = (f32[10,18,1]{2,1,0:T(8,128)S(1)}, f32[10,18,1]{2,1,0:T(8,128)S(1)}, u32[]{:S(2)}, u32[]{:S(2)}) collective-permute-start(f32[10,18,1]{2,1,0:T(8,128)S(1)} %get-tuple-element.385), channel_id=1, source_target_pairs={{0,1},{1,2},{2,3},{4,5},{5,6},{6,7},{8,9},{9,10},{10,11},{12,13},{... | collective-permute-start | bytes 2168 | tf_op jit(solution)/shard_map/ppermute | solution.py:27
  87.5 5.9 %collective-permute-start.8 = (f32[10,1,128]{2,1,0:T(1,128)S(1)}, f32[10,1,128]{2,1,0:T(1,128)S(1)}, u32[]{:S(2)}, u32[]{:S(2)}) collective-permute-start(f32[10,1,128]{2,1,0:T(1,128)S(1)} %get-tuple-element.393), channel_id=1, source_target_pairs={{4,0},{8,4},{12,8},{5,1},{9,5},{13,9},{6,2},{10,6},{14,10},{7,3},{... | collective-permute-start | bytes 15368 | tf_op jit(solution)/shard_map/ppermute | solution.py:30
  88.8 5.9 %collective-permute-start.9 = (f32[10,1,128]{2,1,0:T(1,128)S(1)}, f32[10,1,128]{2,1,0:T(1,128)S(1)}, u32[]{:S(2)}, u32[]{:S(2)}) collective-permute-start(f32[10,1,128]{2,1,0:T(1,128)S(1)} %get-tuple-element.392), channel_id=1, source_target_pairs={{0,4},{4,8},{8,12},{1,5},{5,9},{9,13},{2,6},{6,10},{10,14},{3,7},{... | collective-permute-start | bytes 15368 | tf_op jit(solution)/shard_map/ppermute | solution.py:27
  94.8 5.2 %collective-permute-start.10 = (f32[10,18,1]{2,1,0:T(8,128)S(1)}, f32[10,18,1]{2,1,0:T(8,128)S(1)}, u32[]{:S(2)}, u32[]{:S(2)}) collective-permute-start(f32[10,18,1]{2,1,0:T(8,128)S(1)} %get-tuple-element.382), channel_id=1, source_target_pairs={{1,0},{2,1},{3,2},{5,4},{6,5},{7,6},{9,8},{10,9},{11,10},{13,12},{... | collective-permute-start | bytes 2168 | tf_op jit(solution)/shard_map/ppermute | solution.py:30
  96.1 4.0 %collective-permute-start.11 = (f32[10,18,1]{2,1,0:T(8,128)S(1)}, f32[10,18,1]{2,1,0:T(8,128)S(1)}, u32[]{:S(2)}, u32[]{:S(2)}) collective-permute-start(f32[10,18,1]{2,1,0:T(8,128)S(1)} %get-tuple-element.383), channel_id=1, source_target_pairs={{0,1},{1,2},{2,3},{4,5},{5,6},{6,7},{8,9},{9,10},{10,11},{12,13},{... | collective-permute-start | bytes 2168 | tf_op jit(solution)/shard_map/ppermute | solution.py:27
  123.7 7.7 %collective-permute-start.12 = (f32[10,1,128]{2,1,0:T(1,128)S(1)}, f32[10,1,128]{2,1,0:T(1,128)S(1)}, u32[]{:S(2)}, u32[]{:S(2)}) collective-permute-start(f32[10,1,128]{2,1,0:T(1,128)S(1)} %get-tuple-element.391), channel_id=1, source_target_pairs={{4,0},{8,4},{12,8},{5,1},{9,5},{13,9},{6,2},{10,6},{14,10},{7,3},{... | collective-permute-start | bytes 15368 | tf_op jit(solution)/shard_map/ppermute | solution.py:30
  125.0 6.4 %collective-permute-start.13 = (f32[10,1,128]{2,1,0:T(1,128)S(1)}, f32[10,1,128]{2,1,0:T(1,128)S(1)}, u32[]{:S(2)}, u32[]{:S(2)}) collective-permute-start(f32[10,1,128]{2,1,0:T(1,128)S(1)} %get-tuple-element.390), channel_id=1, source_target_pairs={{0,4},{4,8},{8,12},{1,5},{5,9},{9,13},{2,6},{6,10},{10,14},{3,7},{... | collective-permute-start | bytes 15368 | tf_op jit(solution)/shard_map/ppermute | solution.py:27
  131.5 6.0 %collective-permute-start.14 = (f32[10,18,1]{2,1,0:T(8,128)S(1)}, f32[10,18,1]{2,1,0:T(8,128)S(1)}, u32[]{:S(2)}, u32[]{:S(2)}) collective-permute-start(f32[10,18,1]{2,1,0:T(8,128)S(1)} %get-tuple-element.380), channel_id=1, source_target_pairs={{1,0},{2,1},{3,2},{5,4},{6,5},{7,6},{9,8},{10,9},{11,10},{13,12},{... | collective-permute-start | bytes 2168 | tf_op jit(solution)/shard_map/ppermute | solution.py:30
  132.8 4.7 %collective-permute-start.15 = (f32[10,18,1]{2,1,0:T(8,128)S(1)}, f32[10,18,1]{2,1,0:T(8,128)S(1)}, u32[]{:S(2)}, u32[]{:S(2)}) collective-permute-start(f32[10,18,1]{2,1,0:T(8,128)S(1)} %get-tuple-element.381), channel_id=1, source_target_pairs={{0,1},{1,2},{2,3},{4,5},{5,6},{6,7},{8,9},{9,10},{10,11},{12,13},{... | collective-permute-start | bytes 2168 | tf_op jit(solution)/shard_map/ppermute | solution.py:27
  159.7 7.8 %collective-permute-start.16 = (f32[10,1,128]{2,1,0:T(1,128)S(1)}, f32[10,1,128]{2,1,0:T(1,128)S(1)}, u32[]{:S(2)}, u32[]{:S(2)}) collective-permute-start(f32[10,1,128]{2,1,0:T(1,128)S(1)} %get-tuple-element.389), channel_id=1, source_target_pairs={{4,0},{8,4},{12,8},{5,1},{9,5},{13,9},{6,2},{10,6},{14,10},{7,3},{... | collective-permute-start | bytes 15368 | tf_op jit(solution)/shard_map/ppermute | solution.py:30
  161.0 6.5 %collective-permute-start.17 = (f32[10,1,128]{2,1,0:T(1,128)S(1)}, f32[10,1,128]{2,1,0:T(1,128)S(1)}, u32[]{:S(2)}, u32[]{:S(2)}) collective-permute-start(f32[10,1,128]{2,1,0:T(1,128)S(1)} %get-tuple-element.388), channel_id=1, source_target_pairs={{0,4},{4,8},{8,12},{1,5},{5,9},{9,13},{2,6},{6,10},{10,14},{3,7},{... | collective-permute-start | bytes 15368 | tf_op jit(solution)/shard_map/ppermute | solution.py:27
  167.6 5.9 %collective-permute-start.18 = (f32[10,18,1]{2,1,0:T(8,128)S(1)}, f32[10,18,1]{2,1,0:T(8,128)S(1)}, u32[]{:S(2)}, u32[]{:S(2)}) collective-permute-start(f32[10,18,1]{2,1,0:T(8,128)S(1)} %get-tuple-element.378), channel_id=1, source_target_pairs={{1,0},{2,1},{3,2},{5,4},{6,5},{7,6},{9,8},{10,9},{11,10},{13,12},{... | collective-permute-start | bytes 2168 | tf_op jit(solution)/shard_map/ppermute | solution.py:30
  168.9 4.6 %collective-permute-start.19 = (f32[10,18,1]{2,1,0:T(8,128)S(1)}, f32[10,18,1]{2,1,0:T(8,128)S(1)}, u32[]{:S(2)}, u32[]{:S(2)}) collective-permute-start(f32[10,18,1]{2,1,0:T(8,128)S(1)} %get-tuple-element.379), channel_id=1, source_target_pairs={{0,1},{1,2},{2,3},{4,5},{5,6},{6,7},{8,9},{9,10},{10,11},{12,13},{... | collective-permute-start | bytes 2168 | tf_op jit(solution)/shard_map/ppermute | solution.py:27
